TPU v7x, 64 devices: a 2x2x8 block of a 4x4x8 slice. The times are simulated.
64 devices in a mesh: dp: 8 (over x, y, core), tp: 8 (over z).
Axes of the slice: x: 2, y: 2, z: 8, core: 2. Of those that a mesh axis runs over, the one named last changes fastest.
The devices are a block of a 4x4x8 slice.
Arguments:
- x: bfloat16 [16384, 3584], P('dp'), parts along dimension 0
- w_gate: bfloat16 [3584, 14336], P(None, 'tp')
- w_up: bfloat16 [3584, 14336], P(None, 'tp')
- w_down: bfloat16 [14336, 3584], P('tp')
Outputs:
- output: bfloat16 [16384, 3584], P('dp'), parts along dimension 0
There are 8 independent parts. A program takes and returns all parts, laid end to end along the dimension named above; an argument that names none is the same for every part.
All inputs are finite; a program needn't handle non-finite values.
Results may differ from a plain program's by a relative error of at most 0.016.
Values are sent between devices in bfloat16 or wider.
A program may use at most 768 MiB of HBM per device.

v0:
```python
import jax
import jax.numpy as jnp
from jax import lax
from jax.sharding import PartitionSpec as P


def solution(mesh):
    def step(x, w_gate, w_up, w_down):
        gate = jnp.dot(x, w_gate, preferred_element_type=jnp.float32)
        up = jnp.dot(x, w_up, preferred_element_type=jnp.float32)
        hidden = (jax.nn.gelu(gate) * up).astype(jnp.bfloat16)
        term = jnp.dot(hidden, w_down, preferred_element_type=jnp.float32).astype(jnp.bfloat16)
        return lax.psum(term, "tp")

    return jax.shard_map(
        step,
        mesh=mesh,
        in_specs=(P("dp", None), P(None, "tp"), P(None, "tp"), P("tp", None)),
        out_specs=P("dp", None),
        check_vma=False,
    )
```

profile of v0, /device:TPU:21, one launch (start us, length us, event | category | flops | bytes accessed | tf_op | source)
XLA Modules:
  0.0 436.7 jit_solution(7888089553642143079)
XLA Ops:
  6.5 0.0 all-reduce.2.cloned.1.call-start
  6.6 0.0 copy-start
  6.6 34.9 %fusion.9 = f32[2048,1792]{1,0:T(8,128)} fusion(bf16[2048,3584]{1,0:T(8,128)(2,1)} %param.4, bf16[3584,1792]{1,0:T(8,128)(2,1)} %param.5), kind=kOutput, calls=%fused_computation.11 | convolution fusion | flops 26306674688 | bytes 42205184 | tf_op jit(solution)/shard_map/dot_general | solution.py:9
  41.5 0.0 copy-done
  41.5 36.7 %fusion.8 = bf16[2048,1792]{1,0:T(8,128)(2,1)} fusion(f32[2048,1792]{1,0:T(8,128)} %fusion.9, bf16[2048,3584]{1,0:T(8,128)(2,1)S(1)} %copy-done, bf16[3584,1792]{1,0:T(8,128)(2,1)} %param.6), kind=kOutput, calls=%fused_computation.10 | convolution fusion | flops 26343374848 | bytes 49545216 | tf_op jit(solution)/shard_map/dot_general | solution.py:10
  78.1 34.3 %convolution_convert_fusion = bf16[2048,3584]{1,0:T(8,128)(2,1)} fusion(bf16[2048,1792]{1,0:T(8,128)(2,1)} %fusion.8, bf16[1792,3584]{1,0:T(8,128)(2,1)} %param.7), kind=kOutput, calls=%fused_computation.1 | convolution fusion | flops 26314014720 | bytes 34865152 | tf_op jit(solution)/shard_map/dot_general | solution.py:12
  112.4 0.1 all-reduce.2.cloned.1.call-update
  112.4 304.3 %all-reduce.2.cloned.1.call-done = bf16[2048,3584]{1,0:T(8,128)(2,1)} async-done(((bf16[2048,3584]{1,0:T(8,128)(2,1)}), bf16[2048,3584]{1,0:T(8,128)(2,1)}) %all-reduce.2.cloned.1.call-update) | async-done | bytes 14680080 | tf_op jit(solution)/shard_map/psum | solution.py:13
  416.7 13.1 %copy.6 = bf16[2048,3584]{1,0:T(8,128)(2,1)} copy(bf16[2048,3584]{1,0:T(8,128)(2,1)} %all-reduce.2.cloned.1.call-done) | data formatting | bytes 29360128
Async XLA Ops:
  6.5 410.1 %all-reduce.2.cloned.1.call-start = ((), (), s32[]{:S(2)}) async-start(), calls=%async_computation | async-start | bytes 29360128 | tf_op jit(solution)/shard_map/psum | solution.py:13
  6.6 34.9 %copy-start = (bf16[2048,3584]{1,0:T(8,128)(2,1)S(1)}, bf16[2048,3584]{1,0:T(8,128)(2,1)}, u32[]{:S(2)}) copy-start(bf16[2048,3584]{1,0:T(8,128)(2,1)} %param.4) | copy-start | bytes 44040196
Sparse Core Ops, SparseCore 0:
  112.5 304.0 all-reduce.1
where the time goes:
time: 437 us
  waiting for transfers between devices  304 us (70%)
  matrix products  106 us (24%)
  between operations  13.4 us (3%)
  local copies, waits for them, and re-layouts  13.1 us (3%)
    psum x1, waiting for transfers between devices, step(): return lax.psum(term, 'tp')  304 us
    dot_general x1, matrix products, step(): up = jnp.dot(x, w_up, preferred_element_type=jnp.float32)  36.7 us
    dot_general x1, matrix products, step(): gate = jnp.dot(x, w_gate, preferred_element_type=jnp.float32)  34.9 us
    dot_general x1, matrix products, step(): jnp.dot(hidden, w_down, preferred_element_type=jnp.float32)  34.3 us
    unnamed x3, local copies, waits for them, and re-layouts  13.1 us
  transfers between devices with their start and end apart: 1, of which 1 were waited for; matrix products, arithmetic and copies ran while one was open for 0% of the time, Pallas kernels for 0%

commit v1 on v0

v1 whole, which is shorter than its diff:
```python
import functools

import jax
import jax.numpy as jnp
from jax import lax
from jax.experimental import pallas as pl
from jax.experimental.pallas import tpu as pltpu
from jax.sharding import PartitionSpec as P

MESH = pl.DeviceIdType.MESH
PIECES = 7
CW, CCW = 0, 1


def kernel(n, x_hbm, wg_hbm, wu_hbm, wd_hbm, y_hbm, wgu, wd, xb, hid, buf,
           wgu_sem, wd_sem, x_sem, rs_recv, ag_recv, rs_send, ag_send, own_sem):
    me = lax.axis_index("tp")
    right, left = lax.rem(me + 1, n), lax.rem(me + n - 1, n)
    target = ({"tp": right}, {"tp": left})
    chunk = x_hbm.shape[0] // n
    half = chunk // 2
    fb = wgu.shape[2] // 2
    db = wd.shape[2]

    def rows(d, c):
        return pl.ds(pl.multiple_of(c * chunk + d * half, half), half)

    def rs_chunk(d, k):
        return lax.rem(me + (2 * n - 1 - k if d == CW else 1 + k), n)

    def ag_chunk(d, m):
        return lax.rem(me + (2 * n - m if d == CW else m), n)

    def cols(j):
        return pl.ds(pl.multiple_of(j * db, db), db)

    def x_copy(d, k):
        slot = lax.rem(k, 2)
        return pltpu.make_async_copy(
            x_hbm.at[rows(d, rs_chunk(d, k))], xb.at[slot, pl.ds(d * half, half)], x_sem.at[slot, d])

    def gu_copies(j):
        c = pl.ds(pl.multiple_of(j * fb, fb), fb)
        return (pltpu.make_async_copy(wg_hbm.at[:, c], wgu.at[j, :, pl.ds(0, fb)], wgu_sem.at[0, j]),
                pltpu.make_async_copy(wu_hbm.at[:, c], wgu.at[j, :, pl.ds(fb, fb)], wgu_sem.at[1, j]))

    def wd_copy(j):
        return pltpu.make_async_copy(wd_hbm.at[:, cols(j)], wd.at[j], wd_sem.at[j])

    def rs_copy(d, k, j):
        return pltpu.make_async_remote_copy(
            src_ref=buf.at[d, k, j], dst_ref=buf.at[d, k + 1, j],
            send_sem=rs_send.at[d], recv_sem=rs_recv.at[d, k + 1, j],
            device_id=target[d], device_id_type=MESH)

    def rs_wait(d, k, j):
        pltpu.make_async_copy(buf.at[d, k, j], buf.at[d, k, j], rs_recv.at[d, k, j]).wait()

    def y_piece(d, m, j):
        return y_hbm.at[rows(d, ag_chunk(d, m)), cols(j)]

    def ag_copy(d, m, j, src):
        return pltpu.make_async_remote_copy(
            src_ref=src, dst_ref=y_piece(d, m, j),
            send_sem=ag_send.at[d], recv_sem=ag_recv.at[d, m + 1, j],
            device_id=target[d], device_id_type=MESH)

    def own_copy(d, j):
        return pltpu.make_async_copy(buf.at[d, n - 1, j], y_piece(d, 0, j), own_sem.at[d, j])

    def gate_up(slot, j):
        gu = jnp.dot(xb[slot], wgu[j], preferred_element_type=jnp.float32)
        h = jax.nn.gelu(gu[:, :fb]) * gu[:, fb:]
        hid[slot, :, pl.ds(pl.multiple_of(j * fb, fb), fb)] = h.astype(hid.dtype)

    def down(k, j, first):
        acc = jnp.dot(hid[lax.rem(k, 2)], wd[j], preferred_element_type=jnp.float32)
        for d in (CW, CCW):
            part = acc[d * half:(d + 1) * half]
            if not first:
                rs_wait(d, k, j)
                part = part + buf[d, k, j].astype(jnp.float32)
            buf[d, k, j] = part.astype(buf.dtype)

    for d in (CW, CCW):
        x_copy(d, 0).start()
    for j in range(PIECES):
        for c in gu_copies(j):
            c.start()
    for j in range(PIECES):
        wd_copy(j).start()
    for d in (CW, CCW):
        x_copy(d, 1).start()
    barrier = pltpu.get_barrier_semaphore()
    for d in (CW, CCW):
        pl.semaphore_signal(barrier, inc=1, device_id=target[d], device_id_type=MESH)

    for d in (CW, CCW):
        x_copy(d, 0).wait()

    def prologue(j, _):
        for c in gu_copies(j):
            c.wait()
        gate_up(0, j)
        return 0

    lax.fori_loop(0, PIECES, prologue, 0)
    pl.semaphore_wait(barrier, 2)

    def step(k, first):
        nxt = lax.rem(k + 1, 2)
        for d in (CW, CCW):
            x_copy(d, k + 1).wait()

        def piece(j, _):
            if first:
                wd_copy(j).wait()
            down(k, j, first)
            for d in (CW, CCW):
                rs_copy(d, k, j).start()
            gate_up(nxt, j)
            return 0

        lax.fori_loop(0, PIECES, piece, 0)

    step(0, True)

    def middle(k, _):
        for d in (CW, CCW):
            x_copy(d, k + 1).start()
        step(k, False)
        return 0

    lax.fori_loop(1, n - 1, middle, 0)

    def last(j, _):
        down(n - 1, j, False)
        for d in (CW, CCW):
            ag_copy(d, 0, j, buf.at[d, n - 1, j]).start()
            own_copy(d, j).start()
        return 0

    lax.fori_loop(0, PIECES, last, 0)

    def ag_wait(d, m, j):
        pltpu.make_async_copy(y_piece(d, m, j), y_piece(d, m, j), ag_recv.at[d, m, j]).wait()

    def gather(m, forward):
        def piece(j, _):
            for d in (CW, CCW):
                ag_wait(d, m, j)
                if forward:
                    ag_copy(d, m, j, y_piece(d, m, j)).start()
            return 0

        lax.fori_loop(0, PIECES, piece, 0)

    def gather_forward(m, _):
        gather(m, True)
        return 0

    lax.fori_loop(1, n - 1, gather_forward, 0)
    gather(n - 1, False)

    for d in (CW, CCW):
        sent = buf.at[d, pl.ds(0, n - 1)]
        pltpu.make_async_copy(sent, sent, rs_send.at[d]).wait()
        sent = y_hbm.at[pl.ds(0, (n - 1) * half)]
        pltpu.make_async_copy(sent, sent, ag_send.at[d]).wait()
        for j in range(PIECES):
            own_copy(d, j).wait()


def solution(mesh):
    n = mesh.shape["tp"]

    def step(x, w_gate, w_up, w_down):
        (rows, depth), width = x.shape, w_gate.shape[1]
        half = rows // n // 2
        fb, db = width // PIECES, depth // PIECES
        any_space = pl.BlockSpec(memory_space=pl.ANY)
        return pl.pallas_call(
            functools.partial(kernel, n),
            out_shape=jax.ShapeDtypeStruct((rows, depth), jnp.bfloat16),
            in_specs=[any_space] * 4,
            out_specs=any_space,
            scratch_shapes=[
                pltpu.VMEM((PIECES, depth, 2 * fb), jnp.bfloat16),
                pltpu.VMEM((PIECES, width, db), jnp.bfloat16),
                pltpu.VMEM((2, 2 * half, depth), jnp.bfloat16),
                pltpu.VMEM((2, 2 * half, width), jnp.bfloat16),
                pltpu.VMEM((2, n, PIECES, half, db), jnp.bfloat16),
                pltpu.SemaphoreType.DMA((2, PIECES)),
                pltpu.SemaphoreType.DMA((PIECES,)),
                pltpu.SemaphoreType.DMA((2, 2)),
                pltpu.SemaphoreType.DMA((2, n, PIECES)),
                pltpu.SemaphoreType.DMA((2, n, PIECES)),
                pltpu.SemaphoreType.DMA((2,)),
                pltpu.SemaphoreType.DMA((2,)),
                pltpu.SemaphoreType.DMA((2, PIECES)),
            ],
            cost_estimate=pl.CostEstimate(
                flops=6 * rows * depth * width,
                bytes_accessed=2 * (3 * depth * width + 4 * rows * depth),
                transcendentals=rows * width),
            compiler_params=pltpu.CompilerParams(
                collective_id=0, has_side_effects=True, vmem_limit_bytes=66_000_000),
        )(x, w_gate, w_up, w_down)

    return jax.shard_map(
        step,
        mesh=mesh,
        in_specs=(P("dp", None), P(None, "tp"), P(None, "tp"), P("tp", None)),
        out_specs=P("dp", None),
        check_vma=False,
    )
```

time: 437 us -> 318 us (0.73)
  Pallas kernels: 0 us -> 304 us
  waiting for transfers between devices: 304 us -> 0 us
  matrix products: 106 us -> 0 us
  between operations: 13.4 us -> 0.01 us
    pallas_call x0 -> x1, Pallas kernels: none -> 304 us  [step(): pl.pallas_call(functools.partial(kernel, n), out_shape=jax.ShapeDtypeStru...]
    psum x1 -> x0, waiting for transfers between devices: 304 us -> none  [step(): return lax.psum(term, 'tp')]
    dot_general x3 -> x0, matrix products: 106 us -> none  [the longest x1 36.7 us: step(): up = jnp.dot(x, w_up, preferred_element_type=jnp.float32)]
    unnamed x3 -> x1, local copies, waits for them, and re-layouts: 13.1 us -> 13.1 us
  transfers between devices with their start and end apart: 1 -> 0, of which waited for: 1 -> 0; matrix products, arithmetic and copies ran while one was open for 0% -> 0% of each run, Pallas kernels for 0% -> 0%
where the time goes in v1:
time: 318 us; the launch traced here: 317 us
  Pallas kernels  304 us (96%)
  local copies, waits for them, and re-layouts  13.1 us (4%)
    pallas_call x1, Pallas kernels, step(): pl.pallas_call(functools.partial(kernel, n), out_shape=jax.ShapeDtypeStru...  304 us
    unnamed x1, local copies, waits for them, and re-layouts  13.1 us

profile of v1, /device:TPU:21, one launch (start us, length us, event | category | flops | bytes accessed | tf_op | source)
XLA Modules:
  0.0 317.5 jit_solution(10279737212649957601)
XLA Ops:
  0.0 304.3 %shard_map.46 = bf16[2048,3584]{1,0:T(8,128)(2,1)} custom-call(bf16[2048,3584]{1,0:T(8,128)(2,1)} %x_hbm.1, bf16[3584,1792]{1,0:T(8,128)(2,1)} %wg_hbm.1, bf16[3584,1792]{1,0:T(8,128)(2,1)} %wu_hbm.1, bf16[1792,3584]{1,0:T(8,128)(2,1)} %wd_hbm.1), custom_call_target="tpu_custom_call" | custom-call | flops 78920024064 | bytes 97255424 | tf_op jit(solution)/shard_map/pallas_call | solution.py:182
  304.4 13.1 %copy.6 = bf16[2048,3584]{1,0:T(8,128)(2,1)} copy(bf16[2048,3584]{1,0:T(8,128)(2,1)} %shard_map.46) | data formatting | bytes 29360128

commit v2 on v1

v2 whole, which is shorter than its diff:
```python
import functools

import jax
import jax.numpy as jnp
from jax import lax
from jax.experimental import pallas as pl
from jax.experimental.pallas import tpu as pltpu
from jax.sharding import PartitionSpec as P

MESH = pl.DeviceIdType.MESH
PIECES = 7
AHEAD = 3
CW, CCW = 0, 1


def kernel(n, x_hbm, wg_hbm, wu_hbm, wd_hbm, buf, wgu, wd, xb, hid,
           wgu_sem, wd_sem, x_sem, rs_recv, ag_recv, rs_send, ag_send):
    me = lax.axis_index("tp")
    right, left = lax.rem(me + 1, n), lax.rem(me + n - 1, n)
    target = ({"tp": right}, {"tp": left})
    chunk = x_hbm.shape[0] // n
    half = chunk // 2
    fb = wgu.shape[2] // 2
    db = wd.shape[2]

    def rows(d, c):
        return pl.ds(pl.multiple_of(c * chunk + d * half, half), half)

    def rs_chunk(d, k):
        return lax.rem(me + (2 * n - 1 - k if d == CW else 1 + k), n)

    def ag_chunk(d, m):
        return lax.rem(me + (2 * n - m if d == CW else m), n)

    def cols(j):
        return pl.ds(pl.multiple_of(j * db, db), db)

    def x_copy(d, k):
        slot = lax.rem(k, 2)
        return pltpu.make_async_copy(
            x_hbm.at[rows(d, rs_chunk(d, k))], xb.at[slot, pl.ds(d * half, half)], x_sem.at[slot, d])

    def gu_copies(j):
        c = pl.ds(pl.multiple_of(j * fb, fb), fb)
        return (pltpu.make_async_copy(wg_hbm.at[:, c], wgu.at[j, :, pl.ds(0, fb)], wgu_sem.at[0, j]),
                pltpu.make_async_copy(wu_hbm.at[:, c], wgu.at[j, :, pl.ds(fb, fb)], wgu_sem.at[1, j]))

    def wd_copy(j):
        return pltpu.make_async_copy(wd_hbm.at[:, cols(j)], wd.at[j], wd_sem.at[j])

    def rs_copy(d, k, j):
        piece = buf.at[d, rs_chunk(d, k), j]
        return pltpu.make_async_remote_copy(
            src_ref=piece, dst_ref=piece,
            send_sem=rs_send.at[d, j], recv_sem=rs_recv.at[d, k + 1, j],
            device_id=target[d], device_id_type=MESH)

    def rs_wait(d, k, j):
        piece = buf.at[d, rs_chunk(d, k), j]
        pltpu.make_async_copy(piece, piece, rs_recv.at[d, k, j]).wait()

    def ag_copy(d, m, j):
        piece = buf.at[d, ag_chunk(d, m), j]
        return pltpu.make_async_remote_copy(
            src_ref=piece, dst_ref=piece,
            send_sem=ag_send.at[d], recv_sem=ag_recv.at[d, m + 1, j],
            device_id=target[d], device_id_type=MESH)

    def ag_wait(d, m, j):
        piece = buf.at[d, ag_chunk(d, m), j]
        pltpu.make_async_copy(piece, piece, ag_recv.at[d, m, j]).wait()

    def gate_up(slot, j):
        gu = jnp.dot(xb[slot], wgu[j], preferred_element_type=jnp.float32)
        h = jax.nn.gelu(gu[:, :fb]) * gu[:, fb:]
        hid[slot, :, pl.ds(pl.multiple_of(j * fb, fb), fb)] = h.astype(hid.dtype)

    def down(k, j, first):
        acc = jnp.dot(hid[lax.rem(k, 2)], wd[j], preferred_element_type=jnp.float32)
        for d in (CW, CCW):
            c = rs_chunk(d, k)
            part = acc[d * half:(d + 1) * half]
            if not first:
                rs_wait(d, k, j)
                part = part + buf[d, c, j].astype(jnp.float32)
            buf[d, c, j] = part.astype(buf.dtype)

    def start_gu(j):
        for c in gu_copies(j):
            c.start()

    def start_x(k):
        for d in (CW, CCW):
            x_copy(d, k).start()

    start_x(0)
    for j in range(AHEAD):
        start_gu(j)
    barrier = pltpu.get_barrier_semaphore()
    for d in (CW, CCW):
        pl.semaphore_signal(barrier, inc=1, device_id=target[d], device_id_type=MESH)

    for d in (CW, CCW):
        x_copy(d, 0).wait()

    def prologue(j, _):
        @pl.when(j < PIECES - AHEAD)
        def _():
            start_gu(j + AHEAD)

        @pl.when(j >= PIECES - AHEAD)
        def _():
            wd_copy(j - (PIECES - AHEAD)).start()

        for c in gu_copies(j):
            c.wait()
        gate_up(0, j)
        return 0

    lax.fori_loop(0, PIECES, prologue, 0)
    start_x(1)
    for j in range(AHEAD, PIECES):
        wd_copy(j).start()
    pl.semaphore_wait(barrier, 2)

    def sent(k, j):
        for d in (CW, CCW):
            rs_copy(d, k, j).wait_send()

    def step(k, first):
        def piece(j, _):
            if first:
                wd_copy(j).wait()
            down(k, j, first)
            if not first:
                sent(k - 1, j)
            for d in (CW, CCW):
                rs_copy(d, k, j).start()

            @pl.when(j == 0)
            def _():
                for d in (CW, CCW):
                    x_copy(d, k + 1).wait()

            gate_up(lax.rem(k + 1, 2), j)
            return 0

        lax.fori_loop(0, PIECES, piece, 0)

    step(0, True)

    def middle(k, _):
        start_x(k + 1)
        step(k, False)
        return 0

    lax.fori_loop(1, n - 1, middle, 0)

    def last(j, _):
        down(n - 1, j, False)
        sent(n - 2, j)
        for d in (CW, CCW):
            ag_copy(d, 0, j).start()
        return 0

    lax.fori_loop(0, PIECES, last, 0)

    def gather(m, forward):
        def piece(j, _):
            for d in (CW, CCW):
                ag_wait(d, m, j)
                if forward:
                    ag_copy(d, m, j).start()
            return 0

        lax.fori_loop(0, PIECES, piece, 0)

    def gather_forward(m, _):
        gather(m, True)
        return 0

    lax.fori_loop(1, n - 1, gather_forward, 0)
    gather(n - 1, False)

    for d in (CW, CCW):
        pieces = buf.at[d, pl.ds(0, n - 1)]
        pltpu.make_async_copy(pieces, pieces, ag_send.at[d]).wait()


def unpack(n, buf, y_hbm, sem):
    half, db = buf.shape[3:]

    def copy(d, c, j):
        rows = pl.ds(pl.multiple_of(c * 2 * half + d * half, half), half)
        return pltpu.make_async_copy(buf.at[d, c, j], y_hbm.at[rows, pl.ds(j * db, db)], sem)

    def start(c, _):
        for d in (CW, CCW):
            for j in range(PIECES):
                copy(d, c, j).start()
        return 0

    lax.fori_loop(0, n, start, 0)
    pltpu.make_async_copy(y_hbm, y_hbm, sem).wait()


def solution(mesh):
    n = mesh.shape["tp"]

    def step(x, w_gate, w_up, w_down):
        (rows, depth), width = x.shape, w_gate.shape[1]
        half = rows // n // 2
        fb, db = width // PIECES, depth // PIECES
        any_space = pl.BlockSpec(memory_space=pl.ANY)
        packed = pl.pallas_call(
            functools.partial(kernel, n),
            out_shape=pltpu.VMEM((2, n, PIECES, half, db), jnp.bfloat16),
            in_specs=[any_space] * 4,
            out_specs=pl.BlockSpec(memory_space=pltpu.VMEM),
            scratch_shapes=[
                pltpu.VMEM((PIECES, depth, 2 * fb), jnp.bfloat16),
                pltpu.VMEM((PIECES, width, db), jnp.bfloat16),
                pltpu.VMEM((2, 2 * half, depth), jnp.bfloat16),
                pltpu.VMEM((2, 2 * half, width), jnp.bfloat16),
                pltpu.SemaphoreType.DMA((2, PIECES)),
                pltpu.SemaphoreType.DMA((PIECES,)),
                pltpu.SemaphoreType.DMA((2, 2)),
                pltpu.SemaphoreType.DMA((2, n, PIECES)),
                pltpu.SemaphoreType.DMA((2, n, PIECES)),
                pltpu.SemaphoreType.DMA((2, PIECES)),
                pltpu.SemaphoreType.DMA((2,)),
            ],
            cost_estimate=pl.CostEstimate(
                flops=6 * rows * depth * width,
                bytes_accessed=2 * (3 * depth * width + rows * depth),
                transcendentals=rows * width),
            compiler_params=pltpu.CompilerParams(
                collective_id=0, has_side_effects=True, vmem_limit_bytes=50_000_000),
        )(x, w_gate, w_up, w_down)
        return pl.pallas_call(
            functools.partial(unpack, n),
            out_shape=jax.ShapeDtypeStruct((rows, depth), jnp.bfloat16),
            in_specs=[pl.BlockSpec(memory_space=pltpu.VMEM)],
            out_specs=any_space,
            scratch_shapes=[pltpu.SemaphoreType.DMA],
            compiler_params=pltpu.CompilerParams(vmem_limit_bytes=1_000_000),
        )(packed)

    return jax.shard_map(
        step,
        mesh=mesh,
        in_specs=(P("dp", None), P(None, "tp"), P(None, "tp"), P("tp", None)),
        out_specs=P("dp", None),
        check_vma=False,
    )
```

time: 318 us -> 306 us (0.962)
  local copies, waits for them, and re-layouts: 13.1 us -> 0 us
    unnamed x1 -> x0, local copies, waits for them, and re-layouts: 13.1 us -> none
    pallas_call x1 -> x2, Pallas kernels: 304 us -> 306 us  [the longest x1 300 us: step(): pl.pallas_call(functools.partial(kernel, n), out_shape=pltpu.VMEM((2, n,...]
where the time goes in v2:
time: 306 us
  Pallas kernels  306 us (100%)
    pallas_call x1, Pallas kernels, step(): pl.pallas_call(functools.partial(kernel, n), out_shape=pltpu.VMEM((2, n,...  300 us

profile of v2, /device:TPU:21, one launch (start us, length us, event | category | flops | bytes accessed | tf_op | source)
XLA Modules:
  0.0 305.5 jit_solution(12105756995361787469)
XLA Ops:
  0.0 300.4 %shard_map.46.buf = bf16[2,8,7,128,512]{4,3,2,1,0:T(8,128)(2,1)S(1)} custom-call(bf16[2048,3584]{1,0:T(8,128)(2,1)} %x_hbm.1, bf16[3584,1792]{1,0:T(8,128)(2,1)} %wg_hbm.1, bf16[3584,1792]{1,0:T(8,128)(2,1)} %wu_hbm.1, bf16[1792,3584]{1,0:T(8,128)(2,1)} %wd_hbm.1), custom_call_target="tpu_custom_call" | custom-call | flops 78920024064 | bytes 53215232 | tf_op jit(solution)/shard_map/pallas_call | solution.py:215
  300.4 5.1 %shard_map.47 = bf16[2048,3584]{1,0:T(8,128)(2,1)} custom-call(bf16[2,8,7,128,512]{4,3,2,1,0:T(8,128)(2,1)S(1)} %shard_map.46.buf), custom_call_target="tpu_custom_call" | custom-call | tf_op jit(solution)/shard_map/pallas_call | solution.py:240

commit v3 on v2

--- a/solution.py
+++ b/solution.py
@@ -9,11 +9,12 @@
 
 MESH = pl.DeviceIdType.MESH
 PIECES = 7
-AHEAD = 3
+AHEAD = 2
+GROUPS = ((0, 4), (4, 3))
 CW, CCW = 0, 1
 
 
-def kernel(n, x_hbm, wg_hbm, wu_hbm, wd_hbm, buf, wgu, wd, xb, hid,
+def kernel(n, x_hbm, wg_hbm, wu_hbm, wd_hbm, buf, wgu, wd, xb, hid, lead,
            wgu_sem, wd_sem, x_sem, rs_recv, ag_recv, rs_send, ag_send):
     me = lax.axis_index("tp")
     right, left = lax.rem(me + 1, n), lax.rem(me + n - 1, n)
@@ -49,41 +50,47 @@
         return pltpu.make_async_copy(wd_hbm.at[:, cols(j)], wd.at[j], wd_sem.at[j])
 
     def rs_copy(d, k, j):
-        piece = buf.at[d, rs_chunk(d, k), j]
+        piece = buf.at[d, rs_chunk(d, k), :, cols(j)]
         return pltpu.make_async_remote_copy(
             src_ref=piece, dst_ref=piece,
             send_sem=rs_send.at[d, j], recv_sem=rs_recv.at[d, k + 1, j],
             device_id=target[d], device_id_type=MESH)
 
     def rs_wait(d, k, j):
-        piece = buf.at[d, rs_chunk(d, k), j]
+        piece = buf.at[d, rs_chunk(d, k), :, cols(j)]
         pltpu.make_async_copy(piece, piece, rs_recv.at[d, k, j]).wait()
 
-    def ag_copy(d, m, j):
-        piece = buf.at[d, ag_chunk(d, m), j]
+    def ag_block(d, m, g):
+        first, count = GROUPS[g]
+        return buf.at[d, ag_chunk(d, m), :, pl.ds(first * db, count * db)]
+
+    def ag_copy(d, m, g):
+        block = ag_block(d, m, g)
         return pltpu.make_async_remote_copy(
-            src_ref=piece, dst_ref=piece,
-            send_sem=ag_send.at[d], recv_sem=ag_recv.at[d, m + 1, j],
+            src_ref=block, dst_ref=block,
+            send_sem=ag_send.at[d], recv_sem=ag_recv.at[d, m + 1, g],
             device_id=target[d], device_id_type=MESH)
 
-    def ag_wait(d, m, j):
-        piece = buf.at[d, ag_chunk(d, m), j]
-        pltpu.make_async_copy(piece, piece, ag_recv.at[d, m, j]).wait()
+    def ag_wait(d, m, g):
+        block = ag_block(d, m, g)
+        pltpu.make_async_copy(block, block, ag_recv.at[d, m, g]).wait()
 
     def gate_up(slot, j):
         gu = jnp.dot(xb[slot], wgu[j], preferred_element_type=jnp.float32)
         h = jax.nn.gelu(gu[:, :fb]) * gu[:, fb:]
         hid[slot, :, pl.ds(pl.multiple_of(j * fb, fb), fb)] = h.astype(hid.dtype)
 
-    def down(k, j, first):
-        acc = jnp.dot(hid[lax.rem(k, 2)], wd[j], preferred_element_type=jnp.float32)
+    def put(acc, k, j, first):
         for d in (CW, CCW):
             c = rs_chunk(d, k)
             part = acc[d * half:(d + 1) * half]
             if not first:
                 rs_wait(d, k, j)
-                part = part + buf[d, c, j].astype(jnp.float32)
-            buf[d, c, j] = part.astype(buf.dtype)
+                part = part + buf[d, c, :, cols(j)].astype(jnp.float32)
+            buf[d, c, :, cols(j)] = part.astype(buf.dtype)
+
+    def down(k, j, first):
+        put(jnp.dot(hid[lax.rem(k, 2)], wd[j], preferred_element_type=jnp.float32), k, j, first)
 
     def start_gu(j):
         for c in gu_copies(j):
@@ -94,7 +101,9 @@
             x_copy(d, k).start()
 
     start_x(0)
-    for j in range(AHEAD):
+    start_gu(0)
+    wd_copy(0).start()
+    for j in range(1, AHEAD):
         start_gu(j)
     barrier = pltpu.get_barrier_semaphore()
     for d in (CW, CCW):
@@ -102,40 +111,60 @@
 
     for d in (CW, CCW):
         x_copy(d, 0).wait()
+
+    wd_copy(0).wait()
+    lead[...] = jnp.zeros_like(lead)
 
     def prologue(j, _):
         @pl.when(j < PIECES - AHEAD)
         def _():
             start_gu(j + AHEAD)
 
-        @pl.when(j >= PIECES - AHEAD)
-        def _():
-            wd_copy(j - (PIECES - AHEAD)).start()
-
         for c in gu_copies(j):
             c.wait()
+
+        @pl.when(j == PIECES - 1)
+        def _():
+            start_x(1)
+            for i in range(1, PIECES):
+                wd_copy(i).start()
+
         gate_up(0, j)
+        f = pl.ds(pl.multiple_of(j * fb, fb), fb)
+        lead[...] += jnp.dot(hid[0, :, f], wd[0, f], preferred_element_type=jnp.float32)
         return 0
 
     lax.fori_loop(0, PIECES, prologue, 0)
-    start_x(1)
-    for j in range(AHEAD, PIECES):
-        wd_copy(j).start()
     pl.semaphore_wait(barrier, 2)
 
     def sent(k, j):
         for d in (CW, CCW):
             rs_copy(d, k, j).wait_send()
 
-    def step(k, first):
+    def send(k, j):
+        for d in (CW, CCW):
+            rs_copy(d, k, j).start()
+
+    put(lead[...], 0, 0, True)
+    send(0, 0)
+    for d in (CW, CCW):
+        x_copy(d, 1).wait()
+    gate_up(1, 0)
+
+    def first(j, _):
+        wd_copy(j).wait()
+        down(0, j, True)
+        send(0, j)
+        gate_up(1, j)
+        return 0
+
+    lax.fori_loop(1, PIECES, first, 0)
+
+    def step(k):
         def piece(j, _):
-            if first:
-                wd_copy(j).wait()
-            down(k, j, first)
-            if not first:
-                sent(k - 1, j)
-            for d in (CW, CCW):
-                rs_copy(d, k, j).start()
+            down(k, j, False)
+            sent(k - 1, j)
+            send(k, j)
 
             @pl.when(j == 0)
             def _():
@@ -147,33 +176,29 @@
 
         lax.fori_loop(0, PIECES, piece, 0)
 
-    step(0, True)
-
     def middle(k, _):
         start_x(k + 1)
-        step(k, False)
+        step(k)
         return 0
 
     lax.fori_loop(1, n - 1, middle, 0)
 
-    def last(j, _):
-        down(n - 1, j, False)
-        sent(n - 2, j)
-        for d in (CW, CCW):
-            ag_copy(d, 0, j).start()
-        return 0
-
-    lax.fori_loop(0, PIECES, last, 0)
+    for g, (start, count) in enumerate(GROUPS):
+        def last(j, _):
+            down(n - 1, j, False)
+            sent(n - 2, j)
+            return 0
+
+        lax.fori_loop(start, start + count, last, 0)
+        for d in (CW, CCW):
+            ag_copy(d, 0, g).start()
 
     def gather(m, forward):
-        def piece(j, _):
+        for g in range(len(GROUPS)):
             for d in (CW, CCW):
-                ag_wait(d, m, j)
+                ag_wait(d, m, g)
                 if forward:
-                    ag_copy(d, m, j).start()
-            return 0
-
-        lax.fori_loop(0, PIECES, piece, 0)
+                    ag_copy(d, m, g).start()
 
     def gather_forward(m, _):
         gather(m, True)
@@ -188,19 +213,10 @@
 
 
 def unpack(n, buf, y_hbm, sem):
-    half, db = buf.shape[3:]
-
-    def copy(d, c, j):
-        rows = pl.ds(pl.multiple_of(c * 2 * half + d * half, half), half)
-        return pltpu.make_async_copy(buf.at[d, c, j], y_hbm.at[rows, pl.ds(j * db, db)], sem)
-
-    def start(c, _):
-        for d in (CW, CCW):
-            for j in range(PIECES):
-                copy(d, c, j).start()
-        return 0
-
-    lax.fori_loop(0, n, start, 0)
+    half = buf.shape[2]
+    for c in range(n):
+        for d in (CW, CCW):
+            pltpu.make_async_copy(buf.at[d, c], y_hbm.at[pl.ds((2 * c + d) * half, half)], sem).start()
     pltpu.make_async_copy(y_hbm, y_hbm, sem).wait()
 
 
@@ -214,7 +230,7 @@
         any_space = pl.BlockSpec(memory_space=pl.ANY)
         packed = pl.pallas_call(
             functools.partial(kernel, n),
-            out_shape=pltpu.VMEM((2, n, PIECES, half, db), jnp.bfloat16),
+            out_shape=pltpu.VMEM((2, n, half, depth), jnp.bfloat16),
             in_specs=[any_space] * 4,
             out_specs=pl.BlockSpec(memory_space=pltpu.VMEM),
             scratch_shapes=[
@@ -222,11 +238,12 @@
                 pltpu.VMEM((PIECES, width, db), jnp.bfloat16),
                 pltpu.VMEM((2, 2 * half, depth), jnp.bfloat16),
                 pltpu.VMEM((2, 2 * half, width), jnp.bfloat16),
+                pltpu.VMEM((2 * half, db), jnp.float32),
                 pltpu.SemaphoreType.DMA((2, PIECES)),
                 pltpu.SemaphoreType.DMA((PIECES,)),
                 pltpu.SemaphoreType.DMA((2, 2)),
                 pltpu.SemaphoreType.DMA((2, n, PIECES)),
-                pltpu.SemaphoreType.DMA((2, n, PIECES)),
+                pltpu.SemaphoreType.DMA((2, n, len(GROUPS))),
                 pltpu.SemaphoreType.DMA((2, PIECES)),
                 pltpu.SemaphoreType.DMA((2,)),
             ],

time: 306 us -> 303 us (level)
  no operation moved by 1% of the time
where the time goes in v3:
time: 303 us
  Pallas kernels  303 us (100%)
    pallas_call x1, Pallas kernels, step(): pl.pallas_call(functools.partial(kernel, n), out_shape=pltpu.VMEM((2, n,...  298 us

profile of v3, /device:TPU:21, one launch (start us, length us, event | category | flops | bytes accessed | tf_op | source)
XLA Modules:
  0.0 303.3 jit_solution(15281446729187158500)
XLA Ops:
  0.0 298.0 %shard_map.46.buf = bf16[2,8,128,3584]{3,2,1,0:T(8,128)(2,1)S(1)} custom-call(bf16[2048,3584]{1,0:T(8,128)(2,1)} %x_hbm.1, bf16[3584,1792]{1,0:T(8,128)(2,1)} %wg_hbm.1, bf16[3584,1792]{1,0:T(8,128)(2,1)} %wu_hbm.1, bf16[1792,3584]{1,0:T(8,128)(2,1)} %wd_hbm.1), custom_call_target="tpu_custom_call" | custom-call | flops 78920024064 | bytes 53215232 | tf_op jit(solution)/shard_map/pallas_call | solution.py:231
  298.1 5.2 %shard_map.47 = bf16[2048,3584]{1,0:T(8,128)(2,1)} custom-call(bf16[2,8,128,3584]{3,2,1,0:T(8,128)(2,1)S(1)} %shard_map.46.buf), custom_call_target="tpu_custom_call" | custom-call | tf_op jit(solution)/shard_map/pallas_call | solution.py:257

commit v4 on v3

--- a/solution.py
+++ b/solution.py
@@ -10,15 +10,19 @@
 MESH = pl.DeviceIdType.MESH
 PIECES = 7
 AHEAD = 2
+SHARED = 2
 GROUPS = ((0, 4), (4, 3))
 CW, CCW = 0, 1
 
 
 def kernel(n, x_hbm, wg_hbm, wu_hbm, wd_hbm, buf, wgu, wd, xb, hid, lead,
-           wgu_sem, wd_sem, x_sem, rs_recv, ag_recv, rs_send, ag_send):
+           wgu_sem, wd_sem, x_sem, rs_recv, ag_recv, rs_send, ag_send, pair_send):
     me = lax.axis_index("tp")
     right, left = lax.rem(me + 1, n), lax.rem(me + n - 1, n)
     target = ({"tp": right}, {"tp": left})
+    group = lax.axis_index("dp")
+    side = lax.rem(group, 2)
+    pair = {"dp": group + 1 - 2 * side}
     chunk = x_hbm.shape[0] // n
     half = chunk // 2
     fb = wgu.shape[2] // 2
@@ -45,6 +49,24 @@
         c = pl.ds(pl.multiple_of(j * fb, fb), fb)
         return (pltpu.make_async_copy(wg_hbm.at[:, c], wgu.at[j, :, pl.ds(0, fb)], wgu_sem.at[0, j]),
                 pltpu.make_async_copy(wu_hbm.at[:, c], wgu.at[j, :, pl.ds(fb, fb)], wgu_sem.at[1, j]))
+
+    def half_block(j):
+        return wgu.at[j, :, pl.ds(pl.multiple_of(side * fb, fb), fb)]
+
+    def start_half(j):
+        for i in (0, 1):
+            @pl.when(side == i)
+            def _(i=i):
+                gu_copies(j)[i].start()
+
+    def wait_half(j, i):
+        pltpu.make_async_copy(half_block(j), half_block(j), wgu_sem.at[i, j]).wait()
+
+    def pair_copy(j):
+        return pltpu.make_async_remote_copy(
+            src_ref=half_block(j), dst_ref=half_block(j),
+            send_sem=pair_send.at[j - (PIECES - SHARED)], recv_sem=wgu_sem.at[side, j],
+            device_id=pair, device_id_type=MESH)
 
     def wd_copy(j):
         return pltpu.make_async_copy(wd_hbm.at[:, cols(j)], wd.at[j], wd_sem.at[j])
@@ -100,6 +122,9 @@
         for d in (CW, CCW):
             x_copy(d, k).start()
 
+    shared = range(PIECES - SHARED, PIECES)
+    for j in shared:
+        start_half(j)
     start_x(0)
     start_gu(0)
     wd_copy(0).start()
@@ -108,6 +133,11 @@
     barrier = pltpu.get_barrier_semaphore()
     for d in (CW, CCW):
         pl.semaphore_signal(barrier, inc=1, device_id=target[d], device_id_type=MESH)
+    pl.semaphore_signal(barrier, inc=1, device_id=pair, device_id_type=MESH)
+    pl.semaphore_wait(barrier, 3)
+    for j in shared:
+        wait_half(j, side)
+        pair_copy(j).start()
 
     for d in (CW, CCW):
         x_copy(d, 0).wait()
@@ -116,14 +146,20 @@
     lead[...] = jnp.zeros_like(lead)
 
     def prologue(j, _):
-        @pl.when(j < PIECES - AHEAD)
+        @pl.when(j < PIECES - SHARED - AHEAD)
         def _():
             start_gu(j + AHEAD)
 
-        for c in gu_copies(j):
-            c.wait()
-
-        @pl.when(j == PIECES - 1)
+        @pl.when(j < PIECES - SHARED)
+        def _():
+            for c in gu_copies(j):
+                c.wait()
+
+        @pl.when(j >= PIECES - SHARED)
+        def _():
+            wait_half(j, 1 - side)
+
+        @pl.when(j == PIECES - SHARED)
         def _():
             start_x(1)
             for i in range(1, PIECES):
@@ -135,7 +171,6 @@
         return 0
 
     lax.fori_loop(0, PIECES, prologue, 0)
-    pl.semaphore_wait(barrier, 2)
 
     def sent(k, j):
         for d in (CW, CCW):
@@ -207,6 +242,8 @@
     lax.fori_loop(1, n - 1, gather_forward, 0)
     gather(n - 1, False)
 
+    for j in shared:
+        pair_copy(j).wait_send()
     for d in (CW, CCW):
         pieces = buf.at[d, pl.ds(0, n - 1)]
         pltpu.make_async_copy(pieces, pieces, ag_send.at[d]).wait()
@@ -246,6 +283,7 @@
                 pltpu.SemaphoreType.DMA((2, n, len(GROUPS))),
                 pltpu.SemaphoreType.DMA((2, PIECES)),
                 pltpu.SemaphoreType.DMA((2,)),
+                pltpu.SemaphoreType.DMA((SHARED,)),
             ],
             cost_estimate=pl.CostEstimate(
                 flops=6 * rows * depth * width,

time: 303 us -> 304 us (level)
  no operation moved by 1% of the time
where the time goes in v4:
time: 304 us
  Pallas kernels  304 us (100%)
    pallas_call x1, Pallas kernels, step(): pl.pallas_call(functools.partial(kernel, n), out_shape=pltpu.VMEM((2, n,...  299 us

profile of v4, /device:TPU:21, one launch (start us, length us, event | category | flops | bytes accessed | tf_op | source)
XLA Modules:
  0.0 304.3 jit_solution(15187878400142318160)
XLA Ops:
  0.0 299.1 %shard_map.46.buf = bf16[2,8,128,3584]{3,2,1,0:T(8,128)(2,1)S(1)} custom-call(bf16[2048,3584]{1,0:T(8,128)(2,1)} %x_hbm.1, bf16[3584,1792]{1,0:T(8,128)(2,1)} %wg_hbm.1, bf16[3584,1792]{1,0:T(8,128)(2,1)} %wu_hbm.1, bf16[1792,3584]{1,0:T(8,128)(2,1)} %wd_hbm.1), custom_call_target="tpu_custom_call" | custom-call | flops 78920024064 | bytes 53215232 | tf_op jit(solution)/shard_map/pallas_call | solution.py:268
  299.1 5.2 %shard_map.47 = bf16[2048,3584]{1,0:T(8,128)(2,1)} custom-call(bf16[2,8,128,3584]{3,2,1,0:T(8,128)(2,1)S(1)} %shard_map.46.buf), custom_call_target="tpu_custom_call" | custom-call | tf_op jit(solution)/shard_map/pallas_call | solution.py:295

commit v5 on v3

--- a/solution.py
+++ b/solution.py
@@ -14,13 +14,14 @@
 CW, CCW = 0, 1
 
 
-def kernel(n, x_hbm, wg_hbm, wu_hbm, wd_hbm, buf, wgu, wd, xb, hid, lead,
-           wgu_sem, wd_sem, x_sem, rs_recv, ag_recv, rs_send, ag_send):
+def kernel(n, x_hbm, wg_hbm, wu_hbm, wd_hbm, buf, wgu, wd, xb, hid,
+           wgu_sem, wd_sem, x_sem, x0_sem, rs_recv, ag_recv, rs_send, ag_send):
     me = lax.axis_index("tp")
     right, left = lax.rem(me + 1, n), lax.rem(me + n - 1, n)
     target = ({"tp": right}, {"tp": left})
     chunk = x_hbm.shape[0] // n
     half = chunk // 2
+    quarter = half // 2
     fb = wgu.shape[2] // 2
     db = wd.shape[2]
 
@@ -40,6 +41,12 @@
         slot = lax.rem(k, 2)
         return pltpu.make_async_copy(
             x_hbm.at[rows(d, rs_chunk(d, k))], xb.at[slot, pl.ds(d * half, half)], x_sem.at[slot, d])
+
+    def x0_copy(d, r):
+        start = rs_chunk(d, 0) * chunk + d * half + r * quarter
+        return pltpu.make_async_copy(
+            x_hbm.at[pl.ds(pl.multiple_of(start, quarter), quarter)],
+            xb.at[0, pl.ds((2 * r + d) * quarter, quarter)], x0_sem.at[r, d])
 
     def gu_copies(j):
         c = pl.ds(pl.multiple_of(j * fb, fb), fb)
@@ -75,22 +82,18 @@
         block = ag_block(d, m, g)
         pltpu.make_async_copy(block, block, ag_recv.at[d, m, g]).wait()
 
-    def gate_up(slot, j):
-        gu = jnp.dot(xb[slot], wgu[j], preferred_element_type=jnp.float32)
+    def gate_up(slot, j, rows=slice(None)):
+        gu = jnp.dot(xb[slot, rows], wgu[j], preferred_element_type=jnp.float32)
         h = jax.nn.gelu(gu[:, :fb]) * gu[:, fb:]
-        hid[slot, :, pl.ds(pl.multiple_of(j * fb, fb), fb)] = h.astype(hid.dtype)
-
-    def put(acc, k, j, first):
+        hid[slot, rows, pl.ds(pl.multiple_of(j * fb, fb), fb)] = h.astype(hid.dtype)
+
+    def down(k, j):
+        acc = jnp.dot(hid[lax.rem(k, 2)], wd[j], preferred_element_type=jnp.float32)
         for d in (CW, CCW):
             c = rs_chunk(d, k)
-            part = acc[d * half:(d + 1) * half]
-            if not first:
-                rs_wait(d, k, j)
-                part = part + buf[d, c, :, cols(j)].astype(jnp.float32)
-            buf[d, c, :, cols(j)] = part.astype(buf.dtype)
-
-    def down(k, j, first):
-        put(jnp.dot(hid[lax.rem(k, 2)], wd[j], preferred_element_type=jnp.float32), k, j, first)
+            rs_wait(d, k, j)
+            total = acc[d * half:(d + 1) * half] + buf[d, c, :, cols(j)].astype(jnp.float32)
+            buf[d, c, :, cols(j)] = total.astype(buf.dtype)
 
     def start_gu(j):
         for c in gu_copies(j):
@@ -100,69 +103,86 @@
         for d in (CW, CCW):
             x_copy(d, k).start()
 
-    start_x(0)
-    start_gu(0)
-    wd_copy(0).start()
-    for j in range(1, AHEAD):
+    def start_x0(r):
+        for d in (CW, CCW):
+            x0_copy(d, r).start()
+
+    def wait_x0(r):
+        for d in (CW, CCW):
+            x0_copy(d, r).wait()
+
+    start_x0(0)
+    for j in range(AHEAD):
         start_gu(j)
     barrier = pltpu.get_barrier_semaphore()
     for d in (CW, CCW):
         pl.semaphore_signal(barrier, inc=1, device_id=target[d], device_id_type=MESH)
 
-    for d in (CW, CCW):
-        x_copy(d, 0).wait()
-
-    wd_copy(0).wait()
-    lead[...] = jnp.zeros_like(lead)
+    part = [slice(r * half, (r + 1) * half) for r in (0, 1)]
+    wait_x0(0)
 
     def prologue(j, _):
         @pl.when(j < PIECES - AHEAD)
         def _():
             start_gu(j + AHEAD)
 
+        @pl.when(j >= PIECES - AHEAD)
+        def _():
+            wd_copy(j - (PIECES - AHEAD)).start()
+
+        @pl.when(j == PIECES // 2)
+        def _():
+            start_x0(1)
+
         for c in gu_copies(j):
             c.wait()
-
-        @pl.when(j == PIECES - 1)
-        def _():
-            start_x(1)
-            for i in range(1, PIECES):
-                wd_copy(i).start()
-
-        gate_up(0, j)
-        f = pl.ds(pl.multiple_of(j * fb, fb), fb)
-        lead[...] += jnp.dot(hid[0, :, f], wd[0, f], preferred_element_type=jnp.float32)
+        gate_up(0, j, part[0])
         return 0
 
     lax.fori_loop(0, PIECES, prologue, 0)
+    for j in range(AHEAD, PIECES):
+        wd_copy(j).start()
+    start_x(1)
     pl.semaphore_wait(barrier, 2)
+    wait_x0(1)
+
+    def send(k, j):
+        for d in (CW, CCW):
+            rs_copy(d, k, j).start()
 
     def sent(k, j):
         for d in (CW, CCW):
             rs_copy(d, k, j).wait_send()
 
-    def send(k, j):
-        for d in (CW, CCW):
-            rs_copy(d, k, j).start()
-
-    put(lead[...], 0, 0, True)
-    send(0, 0)
+    def send_part(r, j):
+        acc = jnp.dot(hid[0, part[r]], wd[j], preferred_element_type=jnp.float32)
+        for d in (CW, CCW):
+            piece = buf.at[d, rs_chunk(d, 0), pl.ds(r * quarter, quarter), cols(j)]
+            piece[...] = acc[d * quarter:(d + 1) * quarter].astype(buf.dtype)
+            pltpu.make_async_remote_copy(
+                src_ref=piece, dst_ref=piece,
+                send_sem=rs_send.at[d, j], recv_sem=rs_recv.at[d, 1, j],
+                device_id=target[d], device_id_type=MESH).start()
+
+    def first(j, _):
+        wd_copy(j).wait()
+        send_part(0, j)
+        gate_up(0, j, part[1])
+        return 0
+
+    def second(j, _):
+        send_part(1, j)
+        gate_up(1, j)
+        return 0
+
+    lax.fori_loop(0, PIECES, first, 0)
     for d in (CW, CCW):
         x_copy(d, 1).wait()
-    gate_up(1, 0)
-
-    def first(j, _):
-        wd_copy(j).wait()
-        down(0, j, True)
-        send(0, j)
-        gate_up(1, j)
-        return 0
-
-    lax.fori_loop(1, PIECES, first, 0)
+    lax.fori_loop(0, PIECES, second, 0)
 
     def step(k):
         def piece(j, _):
-            down(k, j, False)
+            down(k, j)
             sent(k - 1, j)
             send(k, j)
 
@@ -185,7 +205,7 @@
 
     for g, (start, count) in enumerate(GROUPS):
         def last(j, _):
-            down(n - 1, j, False)
+            down(n - 1, j)
             sent(n - 2, j)
             return 0
 
@@ -238,9 +258,9 @@
                 pltpu.VMEM((PIECES, width, db), jnp.bfloat16),
                 pltpu.VMEM((2, 2 * half, depth), jnp.bfloat16),
                 pltpu.VMEM((2, 2 * half, width), jnp.bfloat16),
-                pltpu.VMEM((2 * half, db), jnp.float32),
                 pltpu.SemaphoreType.DMA((2, PIECES)),
                 pltpu.SemaphoreType.DMA((PIECES,)),
+                pltpu.SemaphoreType.DMA((2, 2)),
                 pltpu.SemaphoreType.DMA((2, 2)),
                 pltpu.SemaphoreType.DMA((2, n, PIECES)),
                 pltpu.SemaphoreType.DMA((2, n, len(GROUPS))),

time: 303 us -> 302 us (level)
  no operation moved by 1% of the time
where the time goes in v5:
time: 302 us
  Pallas kernels  302 us (100%)
    pallas_call x1, Pallas kernels, step(): pl.pallas_call(functools.partial(kernel, n), out_shape=pltpu.VMEM((2, n,...  297 us

profile of v5, /device:TPU:21, one launch (start us, length us, event | category | flops | bytes accessed | tf_op | source)
XLA Modules:
  0.0 301.7 jit_solution(6723754688469087643)
XLA Ops:
  0.0 296.5 %shard_map.46.buf = bf16[2,8,128,3584]{3,2,1,0:T(8,128)(2,1)S(1)} custom-call(bf16[2048,3584]{1,0:T(8,128)(2,1)} %x_hbm.1, bf16[3584,1792]{1,0:T(8,128)(2,1)} %wg_hbm.1, bf16[3584,1792]{1,0:T(8,128)(2,1)} %wu_hbm.1, bf16[1792,3584]{1,0:T(8,128)(2,1)} %wd_hbm.1), custom_call_target="tpu_custom_call" | custom-call | flops 78920024064 | bytes 53215232 | tf_op jit(solution)/shard_map/pallas_call | solution.py:251
  296.5 5.2 %shard_map.47 = bf16[2048,3584]{1,0:T(8,128)(2,1)} custom-call(bf16[2,8,128,3584]{3,2,1,0:T(8,128)(2,1)S(1)} %shard_map.46.buf), custom_call_target="tpu_custom_call" | custom-call | tf_op jit(solution)/shard_map/pallas_call | solution.py:277

commit v6 on v5

--- a/solution.py
+++ b/solution.py
@@ -126,25 +126,25 @@
         def _():
             start_gu(j + AHEAD)
 
-        @pl.when(j >= PIECES - AHEAD)
-        def _():
-            wd_copy(j - (PIECES - AHEAD)).start()
-
-        @pl.when(j == PIECES // 2)
-        def _():
-            start_x0(1)
+        @pl.when(j == PIECES - AHEAD)
+        def _():
+            wd_copy(0).start()
 
         for c in gu_copies(j):
             c.wait()
+
+        @pl.when(j == PIECES - 1)
+        def _():
+            start_x0(1)
+            for i in range(1, PIECES):
+                wd_copy(i).start()
+            start_x(1)
+
         gate_up(0, j, part[0])
         return 0
 
     lax.fori_loop(0, PIECES, prologue, 0)
-    for j in range(AHEAD, PIECES):
-        wd_copy(j).start()
-    start_x(1)
     pl.semaphore_wait(barrier, 2)
-    wait_x0(1)
 
     def send(k, j):
         for d in (CW, CCW):
@@ -167,6 +167,11 @@
     def first(j, _):
         wd_copy(j).wait()
         send_part(0, j)
+
+        @pl.when(j == 0)
+        def _():
+            wait_x0(1)
+
         gate_up(0, j, part[1])
         return 0
 

time: 302 us -> 302 us (level)
  no operation moved by 1% of the time
where the time goes in v6:
time: 302 us
  Pallas kernels  302 us (100%)
    pallas_call x1, Pallas kernels, step(): pl.pallas_call(functools.partial(kernel, n), out_shape=pltpu.VMEM((2, n,...  297 us

profile of v6, /device:TPU:21, one launch (start us, length us, event | category | flops | bytes accessed | tf_op | source)
XLA Modules:
  0.0 301.8 jit_solution(12639441868313470413)
XLA Ops:
  0.0 296.6 %shard_map.46.buf = bf16[2,8,128,3584]{3,2,1,0:T(8,128)(2,1)S(1)} custom-call(bf16[2048,3584]{1,0:T(8,128)(2,1)} %x_hbm.1, bf16[3584,1792]{1,0:T(8,128)(2,1)} %wg_hbm.1, bf16[3584,1792]{1,0:T(8,128)(2,1)} %wu_hbm.1, bf16[1792,3584]{1,0:T(8,128)(2,1)} %wd_hbm.1), custom_call_target="tpu_custom_call" | custom-call | flops 78920024064 | bytes 53215232 | tf_op jit(solution)/shard_map/pallas_call | solution.py:256
  296.6 5.2 %shard_map.47 = bf16[2048,3584]{1,0:T(8,128)(2,1)} custom-call(bf16[2,8,128,3584]{3,2,1,0:T(8,128)(2,1)S(1)} %shard_map.46.buf), custom_call_target="tpu_custom_call" | custom-call | tf_op jit(solution)/shard_map/pallas_call | solution.py:282
